TPU v7x, 512 devices: a 8x2x16 block of a 8x16x16 slice. The times are simulated.
512 devices in a mesh: groups: 2 (over y), seq: 16 (over z), head: 8 (over x), layer: 2 (over core).
Axes of the slice: x: 8, y: 2, z: 16, core: 2. Of those that a mesh axis runs over, the one named last changes fastest.
The devices are a block of a 8x16x16 slice.
Arguments:
- kv_cache: bfloat16 [2, 2, 8, 16384, 8, 128], P(None, 'layer', 'groups', 'seq', 'head'), parts along dimension 2, may hold values from -800 to 800
- valid_blocks: int32 [8], P('groups'), parts along dimension 0, may hold values from 1 to 128, 256 in all
Outputs:
- decode_cache: bfloat16 [2, 2, 32, 4096, 8, 128], P(None, 'layer', ('groups', 'seq'), None, 'head'), parts along dimension 2
- centers: float32 [2, 2, 8, 8, 128], P(None, 'layer', 'groups', 'head'), parts along dimension 2
- scales: float32 [2, 2, 8, 8, 128], P(None, 'layer', 'groups', 'head'), parts along dimension 2
There are 2 independent parts, one for each index of `groups`. A program takes and returns all parts, laid end to end along the dimension named above; each array names one. Nothing has to cross between parts.
Inputs may be any that keep to these rules, and one draw needn't show every extreme that they name: `valid_blocks`: the counts of the 4 users sum to 256, and the largest equals 128.
All inputs are finite; a program needn't handle non-finite values.
Results may differ from a plain program's by a relative error of at most 0.001.
Values may be sent and summed in bfloat16 or wider, within the bound.
A program may use at most 64 MiB of HBM per device.

v0:
```python
import jax
import jax.numpy as jnp
from jax import lax
from jax.sharding import PartitionSpec as P

BLOCK = 128


epsilon = 1e-06
ceiling_value = 3e38


def from_everyone(array, axis):
    copies = jnp.broadcast_to(array, (lax.axis_size(axis), *array.shape))
    return lax.all_to_all(copies, axis, split_axis=0, concat_axis=0, tiled=True)


def all_in_one(array, axis):
    leaves = jax.tree.leaves(array)
    turns = sorted(range(len(leaves)), key=lambda k: -leaves[k].size)
    width = (1, *leaves[turns[0]].shape)[-1]
    lines = [
        jnp.pad(leaves[k].reshape(-1), (0, -leaves[k].size % width)).reshape(-1, width)
        for k in turns
    ]
    both, at, found = (from_everyone(jnp.concatenate(lines), axis), 0, {})
    for k, line in zip(turns, lines):
        share = both[:, at : at + len(line)].reshape(len(both), -1)
        found[k] = share[:, : leaves[k].size].reshape(-1, *leaves[k].shape)
        at += len(line)
    numbers = iter(range(len(leaves)))
    return jax.tree.map(lambda _: found[next(numbers)], array)


def combined_pairwise(pieces, combine):
    while len(jax.tree.leaves(pieces)[0]) > 1:
        pieces = jax.vmap(combine)(
            *(jax.tree.map(lambda part: part[side::2], pieces) for side in (0, 1))
        )
    return jax.tree.map(lambda part: part[0], pieces)


def joined_all(array, axis, combine):
    pieces = all_in_one(array, axis)
    return combined_pairwise(pieces, combine)


def combine_stats(left_side, right_side):
    return (
        left_side[0] + right_side[0],
        jnp.maximum(left_side[1], right_side[1]),
        jnp.minimum(left_side[2], right_side[2]),
    )


def on_device(kv_cache, valid_blocks):
    kind_count, layer_dev, user_count, per_dev, heads_dev, head_dim = kv_cache.shape
    owners = lax.axis_size("seq")
    quarter = owners // user_count
    part_len = per_dev // quarter
    seq_index = lax.axis_index("seq")
    lengths = valid_blocks * BLOCK
    values = kv_cache.astype(jnp.float32)
    position = seq_index * per_dev + jnp.arange(per_dev, dtype=jnp.int32)
    is_live = position[None, :] < lengths[:, None]
    live_mask = is_live[None, None, :, :, None, None]
    local_sum = jnp.sum(jnp.where(live_mask, values, 0.0), axis=3)
    user_lengths = lengths.astype(jnp.float32)[None, None, :, None, None]
    local_high = jnp.max(jnp.where(live_mask, values, -ceiling_value), axis=3)
    local_low = jnp.min(jnp.where(live_mask, values, ceiling_value), axis=3)
    totals, highest, lowest = joined_all((local_sum, local_high, local_low), "seq", combine_stats)
    centers = totals / user_lengths
    spread = jnp.maximum(highest - centers, centers - lowest)
    scales = spread + epsilon
    normed = jnp.where(
        live_mask, (values - centers[:, :, :, None]) / scales[:, :, :, None], 0.0
    ).astype(jnp.bfloat16)
    outgoing = normed.reshape(
        kind_count, layer_dev, user_count * quarter, part_len, heads_dev, head_dim
    )
    received = lax.all_to_all(outgoing, "seq", split_axis=2, concat_axis=2, tiled=True)
    arranged = received.reshape(kind_count, layer_dev, 1, owners * part_len, heads_dev, head_dim)
    return (arranged, centers, scales)


def solution(mesh):
    in_specs = (P(None, "layer", "groups", "seq", "head", None), P("groups"))
    out_specs = (
        P(None, "layer", ("groups", "seq"), None, "head", None),
        P(None, "layer", "groups", "head", None),
        P(None, "layer", "groups", "head", None),
    )
    return jax.shard_map(
        on_device, mesh=mesh, in_specs=in_specs, out_specs=out_specs, check_vma=False
    )
```

profile of v0, /device:TPU:78, one launch (start us, length us, event | category | flops | bytes accessed | tf_op | source)
XLA Modules:
  0.0 169.0 jit_solution(14551029651689146613)
XLA Ops:
  0.6 0.0 copy-start
  0.6 0.8 fusion.8
  1.5 0.1 broadcast_compare_fusion
  1.5 3.1 %fusion = (f32[2,4,128]{2,1,0:T(4,128)S(1)}, f32[2,4,128]{2,1,0:T(4,128)S(1)}, f32[2,4,128]{2,1,0:T(4,128)S(1)}) fusion(bf16[2,1,4,1024,1,128]{5,3,4,2,1,0:T(8,128)(2,1)} %param.2, pred[4,1024]{1,0:T(4,128)(4,1)S(1)} %broadcast_compare_fusion), kind=kLoop, calls=%fused_computation.4 | loop fusion | flops 7336960 | bytes 2113536 | tf_op jit(solution)/shard_map/reduce_sum | solution.py:67
  4.7 59.7 %all_to_all.10 = f32[16,24,128]{2,1,0:T(8,128)S(1)} all-to-all(f32[16,24,128]{2,1,0:T(8,128)S(1)} %broadcast_in_dim.41), channel_id=1, replica_groups=mesh['groups'=2,'seq'=16,'head'=8,'layer'=2] {'seq'}, dimensions={0} | all-to-all | bytes 393216 | tf_op jit(solution)/shard_map/all_to_all | solution.py:15
  64.5 0.1 fusion.7
  64.6 0.0 copy-done
  64.6 1.0 fusion.5
  65.6 1.5 copy.12
  67.1 5.2 %all-to-all-start.1 = ((bf16[2,1,16,256,1,128]{5,3,0,4,1,2:T(8,128)(2,1)}), bf16[2,1,16,256,1,128]{5,3,0,4,1,2:T(8,128)(2,1)S(1)}, u32[]{:S(2)}, u32[]{:S(2)}) async-start(bf16[2,1,16,256,1,128]{5,3,0,4,1,2:T(8,128)(2,1)} %copy.12), calls=%async_computation.1 | async-start | bytes 4194304 | tf_op jit(solution)/shard_map/all_to_all | solution.py:81
  72.3 0.1 bitcast_subtract_fusion
  72.4 0.0 copy-start.1
  72.4 0.6 maximum_add_fusion
  73.0 94.5 %all-to-all-done.1 = bf16[2,1,16,256,1,128]{5,3,0,4,1,2:T(8,128)(2,1)S(1)} async-done(((bf16[2,1,16,256,1,128]{5,3,0,4,1,2:T(8,128)(2,1)}), bf16[2,1,16,256,1,128]{5,3,0,4,1,2:T(8,128)(2,1)S(1)}, u32[]{:S(2)}, u32[]{:S(2)}) %all-to-all-start.1) | async-done | bytes 2097184 | tf_op jit(solution)/shard_map/all_to_all | solution.py:81
  167.5 1.5 copy.13
  169.0 0.0 copy-done.1
  (12 shorter events, 0.1 us)
Async XLA Ops:
  0.6 63.9 %copy-start = (bf16[2,1,4,1024,1,128]{5,3,4,2,1,0:T(8,128)(2,1)S(1)}, bf16[2,1,4,1024,1,128]{5,3,4,2,1,0:T(8,128)(2,1)}, u32[]{:S(2)}) copy-start(bf16[2,1,4,1024,1,128]{5,3,4,2,1,0:T(8,128)(2,1)} %param.2) | copy-start | bytes 6291460
  67.1 100.4 %all-to-all-start.1 = ((bf16[2,1,16,256,1,128]{5,3,0,4,1,2:T(8,128)(2,1)}), bf16[2,1,16,256,1,128]{5,3,0,4,1,2:T(8,128)(2,1)S(1)}, u32[]{:S(2)}, u32[]{:S(2)}) async-start(bf16[2,1,16,256,1,128]{5,3,0,4,1,2:T(8,128)(2,1)} %copy.12), calls=%async_computation.1 | async-start | bytes 4194304 | tf_op jit(solution)/shard_map/all_to_all | solution.py:81
  72.4 96.7 %copy-start.1 = (f32[2,1,4,1,128]{4,2,0,3,1:T(4,128)}, f32[2,1,4,1,128]{4,2,0,3,1:T(4,128)S(1)}, u32[]{:S(2)}) copy-start(f32[2,1,4,1,128]{4,2,0,3,1:T(4,128)S(1)} %get-tuple-element.16) | copy-start | bytes 12292
where the time goes:
time: 169 us
  waiting for transfers between devices  94.5 us (56%)
  blocking collectives  59.7 us (35%)
  other arithmetic  5.83 us (3%)
  starting transfers between devices  5.24 us (3%)
  local copies, waits for them, and re-layouts  3.05 us (2%)
    all_to_all x1, waiting for transfers between devices, on_device(): lax.all_to_all(outgoing, 'seq', split_axis=2, concat_axis=2, tiled=True)  94.5 us
    all_to_all x1, blocking collectives, from_everyone(): return lax.all_to_all(copies, axis, split_axis=0, concat_axis=0, tiled=True)  59.7 us
    all_to_all x1, starting transfers between devices, on_device(): lax.all_to_all(outgoing, 'seq', split_axis=2, concat_axis=2, tiled=True)  5.24 us
  transfers between devices with their start and end apart: 1, of which 1 were waited for; matrix products, arithmetic and copies ran while one was open for 0% of the time, Pallas kernels for 0%

commit v1 on v0

v1 whole, which is shorter than its diff:
```python
import functools

import jax
import jax.numpy as jnp
from jax import lax
from jax.experimental import pallas as pl
from jax.experimental.pallas import tpu as pltpu
from jax.sharding import PartitionSpec as P

BLOCK = 128

epsilon = 1e-06
ceiling_value = 3e38
ROOT = 0


def exchange_kernel(
    n,
    kv_ref,
    blocks_ref,
    recv_ref,
    finals_ref,
    local,
    mine,
    gathered,
    finals,
    load_sem,
    own_sem,
    send_sem,
    recv_sem,
    stat_send_sem,
    stat_recv_sem,
    final_send_sem,
    final_recv_sem,
    ready,
):
    kinds, owners, part_len, head_dim = kv_ref.shape
    users = blocks_ref.shape[0]
    quarter = owners // users
    per_part = part_len // BLOCK
    per_dev = quarter * per_part
    rows = kinds * users
    z = lax.axis_index("seq")

    load = pltpu.make_async_copy(kv_ref, local, load_sem)
    load.start()

    barrier = pltpu.get_barrier_semaphore()

    @pl.when(z > 0)
    def _():
        pl.semaphore_wait(barrier, 1)

    @pl.when(z < n - 1)
    def _():
        pl.semaphore_signal(barrier, inc=1, device_id={"seq": z + 1})

    def announce(s, carry):
        pl.semaphore_signal(ready.at[z], inc=1, device_id={"seq": s})
        return carry

    lax.fori_loop(0, z, announce, 0)

    def bulk(t):
        return pltpu.make_async_remote_copy(
            src_ref=kv_ref.at[:, t],
            dst_ref=recv_ref.at[:, z],
            send_sem=send_sem.at[t],
            recv_sem=recv_sem.at[z],
            device_id={"seq": t},
        )

    @pl.when(z > 0)
    def _():
        bulk(0).start()

    load.wait()
    own = pltpu.make_async_copy(local.at[:, z], recv_ref.at[:, z], own_sem)
    own.start()

    def one_row(r, carry):
        k, u = r // users, r % users
        total = jnp.zeros((8, head_dim), jnp.float32)
        high = jnp.full((8, head_dim), -ceiling_value, jnp.float32)
        low = jnp.full((8, head_dim), ceiling_value, jnp.float32)
        count = blocks_ref[u]
        for b in range(per_dev):
            part = local[
                k,
                u * quarter + b // per_part,
                (b % per_part) * BLOCK : (b % per_part + 1) * BLOCK,
                :,
            ].astype(jnp.float32)
            part = part.reshape(BLOCK // 8, 8, head_dim)
            alive = z * per_dev + b < count
            total += jnp.where(alive, jnp.sum(part, axis=0), 0.0)
            high = jnp.maximum(high, jnp.where(alive, jnp.max(part, axis=0), -ceiling_value))
            low = jnp.minimum(low, jnp.where(alive, jnp.min(part, axis=0), ceiling_value))
        mine[0, pl.ds(r, 1), :] = jnp.sum(total, axis=0, keepdims=True)
        mine[1, pl.ds(r, 1), :] = jnp.max(high, axis=0, keepdims=True)
        mine[2, pl.ds(r, 1), :] = jnp.min(low, axis=0, keepdims=True)
        return carry

    lax.fori_loop(0, rows, one_row, 0)

    def stat_copy():
        return pltpu.make_async_remote_copy(
            src_ref=mine,
            dst_ref=gathered.at[z],
            send_sem=stat_send_sem,
            recv_sem=stat_recv_sem.at[z],
            device_id={"seq": ROOT},
        )

    @pl.when(z != ROOT)
    def _():
        stat_copy().start()

    def send_lower(t, carry):
        bulk(t).start()
        return carry

    lax.fori_loop(1, z, send_lower, 0)

    def send_upper(t, carry):
        pl.semaphore_wait(ready.at[t], 1)
        bulk(t).start()
        return carry

    lax.fori_loop(z + 1, n, send_upper, 0)

    def final_copy(t):
        return pltpu.make_async_remote_copy(
            src_ref=finals,
            dst_ref=finals,
            send_sem=final_send_sem.at[t],
            recv_sem=final_recv_sem,
            device_id={"seq": t},
        )

    @pl.when(z == ROOT)
    def _():
        def merge(s, carry):
            total, high, low = carry
            pltpu.make_async_remote_copy(
                src_ref=mine,
                dst_ref=gathered.at[s],
                send_sem=stat_send_sem,
                recv_sem=stat_recv_sem.at[s],
                device_id={"seq": ROOT},
            ).wait_recv()
            return (
                total + gathered[s, 0],
                jnp.maximum(high, gathered[s, 1]),
                jnp.minimum(low, gathered[s, 2]),
            )

        total, high, low = lax.fori_loop(1, n, merge, (mine[0], mine[1], mine[2]))
        row = lax.broadcasted_iota(jnp.int32, (rows, head_dim), 0)
        length = jnp.zeros((rows, head_dim), jnp.float32)
        for u in range(users):
            tokens = (blocks_ref[u] * BLOCK).astype(jnp.float32)
            length = jnp.where(row % users == u, tokens, length)
        center = total / length
        finals[0] = center
        finals[1] = jnp.maximum(high - center, center - low) + epsilon

        def send_final(t, carry):
            final_copy(t).start()
            return carry

        lax.fori_loop(1, n, send_final, 0)

        def drain_final(t, carry):
            final_copy(t).wait_send()
            return carry

        lax.fori_loop(1, n, drain_final, 0)

    @pl.when(z != ROOT)
    def _():
        final_copy(0).wait_recv()
        stat_copy().wait_send()

    finals_ref[...] = finals[...]

    def drain(t, carry):
        @pl.when(t != z)
        def _():
            bulk(t).wait_send()
            pltpu.make_async_remote_copy(
                src_ref=kv_ref.at[:, t],
                dst_ref=recv_ref.at[:, t],
                send_sem=send_sem.at[t],
                recv_sem=recv_sem.at[t],
                device_id={"seq": t},
            ).wait_recv()

        return carry

    lax.fori_loop(0, n, drain, 0)
    own.wait()


def on_device(kv_cache, valid_blocks):
    kinds, layer_dev, users, per_dev, heads_dev, head_dim = kv_cache.shape
    n = lax.axis_size("seq")
    quarter = n // users
    part_len = per_dev // quarter
    rows = kinds * users
    kv = kv_cache.reshape(kinds, n, part_len, head_dim)
    recv, finals = pl.pallas_call(
        functools.partial(exchange_kernel, n),
        out_shape=(
            jax.ShapeDtypeStruct((kinds, n, part_len, head_dim), kv.dtype),
            jax.ShapeDtypeStruct((2, rows, head_dim), jnp.float32),
        ),
        in_specs=[
            pl.BlockSpec(memory_space=pl.ANY),
            pl.BlockSpec(memory_space=pltpu.SMEM),
        ],
        out_specs=(
            pl.BlockSpec(memory_space=pl.ANY),
            pl.BlockSpec(memory_space=pltpu.VMEM),
        ),
        scratch_shapes=[
            pltpu.VMEM((kinds, n, part_len, head_dim), kv.dtype),
            pltpu.VMEM((3, rows, head_dim), jnp.float32),
            pltpu.VMEM((n, 3, rows, head_dim), jnp.float32),
            pltpu.VMEM((2, rows, head_dim), jnp.float32),
            pltpu.SemaphoreType.DMA,
            pltpu.SemaphoreType.DMA,
            pltpu.SemaphoreType.DMA((n,)),
            pltpu.SemaphoreType.DMA((n,)),
            pltpu.SemaphoreType.DMA,
            pltpu.SemaphoreType.DMA((n,)),
            pltpu.SemaphoreType.DMA((n,)),
            pltpu.SemaphoreType.DMA,
            pltpu.SemaphoreType.REGULAR((n,)),
        ],
        compiler_params=pltpu.CompilerParams(collective_id=0, has_side_effects=True),
    )(kv, valid_blocks)
    z = lax.axis_index("seq")
    user = z // quarter
    per_row = finals.reshape(2, kinds, users, head_dim)
    mine = lax.dynamic_slice_in_dim(per_row, user, 1, axis=2)[:, :, :, None, :]
    length = lax.dynamic_slice_in_dim(valid_blocks, user, 1)[0] * BLOCK
    source = jnp.arange(n, dtype=jnp.int32)[:, None]
    offset = jnp.arange(part_len, dtype=jnp.int32)[None, :]
    position = source * per_dev + (z % quarter) * part_len + offset
    live = (position < length)[None, :, :, None]
    normed = jnp.where(live, (recv.astype(jnp.float32) - mine[0]) / mine[1], 0.0)
    arranged = normed.astype(kv_cache.dtype).reshape(
        kinds, layer_dev, 1, n * part_len, heads_dev, head_dim
    )
    outs = finals.reshape(2, kinds, layer_dev, users, heads_dev, head_dim)
    return (arranged, outs[0], outs[1])


def solution(mesh):
    in_specs = (P(None, "layer", "groups", "seq", "head", None), P("groups"))
    out_specs = (
        P(None, "layer", ("groups", "seq"), None, "head", None),
        P(None, "layer", "groups", "head", None),
        P(None, "layer", "groups", "head", None),
    )
    return jax.shard_map(
        on_device, mesh=mesh, in_specs=in_specs, out_specs=out_specs, check_vma=False
    )
```

time: 169 us -> 135 us (0.80)
  Pallas kernels: 0 us -> 128 us
  waiting for transfers between devices: 94.5 us -> 0 us
  blocking collectives: 59.7 us -> 0 us
  starting transfers between devices: 5.24 us -> 0 us
  other arithmetic: 5.83 us -> 3.17 us
    pallas_call x0 -> x1, Pallas kernels: none -> 128 us  [on_device(): pl.pallas_call(functools.partial(exchange_kernel, n), out_shape=(jax.Shap...]
    all_to_all x1 -> x0, waiting for transfers between devices: 94.5 us -> none  [on_device(): lax.all_to_all(outgoing, 'seq', split_axis=2, concat_axis=2, tiled=True)]
    all_to_all x1 -> x0, blocking collectives: 59.7 us -> none  [from_everyone(): return lax.all_to_all(copies, axis, split_axis=0, concat_axis=0, tiled=True)]
    all_to_all x1 -> x0, starting transfers between devices: 5.24 us -> none  [on_device(): lax.all_to_all(outgoing, 'seq', split_axis=2, concat_axis=2, tiled=True)]
    reduce_sum x1 -> x0, other arithmetic: 3.11 us -> none  [on_device(): local_sum = jnp.sum(jnp.where(live_mask, values, 0.0), axis=3)]
  transfers between devices with their start and end apart: 1 -> 0, of which waited for: 1 -> 0; matrix products, arithmetic and copies ran while one was open for 0% -> 0% of each run, Pallas kernels for 0% -> 0%
where the time goes in v1:
time: 135 us
  Pallas kernels  128 us (95%)
  other arithmetic  3.17 us (2%)
  local copies, waits for them, and re-layouts  2.54 us (2%)
    pallas_call x1, Pallas kernels, on_device(): pl.pallas_call(functools.partial(exchange_kernel, n), out_shape=(jax.Shap...  128 us
    convert_element_type x1, other arithmetic, on_device(): normed.astype(kv_cache.dtype)  3.09 us

profile of v1, /device:TPU:78, one launch (start us, length us, event | category | flops | bytes accessed | tf_op | source)
XLA Modules:
  0.0 134.9 jit_solution(5293881188512963698)
XLA Ops:
  0.7 1.2 dynamic_slice.6
  2.6 0.1 add_compare_fusion
  2.6 127.9 %shard_map.49 = (bf16[2,16,256,128]{3,2,1,0:T(8,128)(2,1)}, f32[2,8,128]{2,1,0:T(8,128)}) custom-call(bf16[2,16,256,128]{3,2,1,0:T(8,128)(2,1)} %bitcast.14, s32[4]{0:T(128)} %blocks_ref.1), custom_call_target="tpu_custom_call" | custom-call | tf_op jit(solution)/shard_map/pallas_call | solution.py:212
  130.5 0.7 constant_dynamic-slice_fusion
  131.2 0.0 copy-start
  131.2 3.1 %select_convert_fusion = bf16[2,16,256,128]{3,2,1,0:T(8,128)(2,1)} fusion(bf16[2,16,256,128]{3,2,1,0:T(8,128)(2,1)} %get-tuple-element.5, f32[2,128]{1,0:T(2,128)S(1)} %bitcast.18, f32[2,128]{1,0:T(2,128)S(1)} %bitcast.17, pred[16,256]{1,0:T(8,128)(4,1)S(1)} %add_compare_fusion), kind=kLoop, calls=%fused_computation | loop fusion | flops 5242880 | bytes 4200448 | tf_op jit(solution)/shard_map/convert_element_type | solution.py:253
  134.3 0.0 copy-done
  134.3 0.6 fusion
  (1 shorter events, 0.0 us)
Async XLA Ops:
  131.2 3.1 %copy-start = (f32[2,8,128]{2,1,0:T(8,128)S(1)}, f32[2,8,128]{2,1,0:T(8,128)}, u32[]{:S(2)}) copy-start(f32[2,8,128]{2,1,0:T(8,128)} %get-tuple-element.6) | copy-start | bytes 24580

commit v2 on v1

v2 whole, which is shorter than its diff:
```python
import functools

import jax
import jax.numpy as jnp
from jax import lax
from jax.experimental import pallas as pl
from jax.experimental.pallas import tpu as pltpu
from jax.sharding import PartitionSpec as P

BLOCK = 128

epsilon = 1e-06
ceiling_value = 3e38
KEEP = 2


def exchange_kernel(
    n,
    kv_ref,
    blocks_ref,
    out_ref,
    centers_ref,
    scales_ref,
    local,
    recv,
    done,
    mine,
    gathered,
    finals,
    load_sem,
    own_sem,
    out_sem,
    send_sem,
    recv_sem,
    stat_send_sem,
    stat_recv_sem,
    final_send_sem,
    final_recv_sem,
    ready,
    token,
):
    kinds, owners, part_len, head_dim = kv_ref.shape
    users = blocks_ref.shape[0]
    quarter = owners // users
    per_part = part_len // BLOCK
    per_dev = quarter * per_part
    rows = kinds * users
    half = n // 2
    z = lax.axis_index("seq")
    my_user, my_part = z // quarter, z % quarter
    early = z < half

    load = pltpu.make_async_copy(kv_ref, local, load_sem)
    load.start()
    own = pltpu.make_async_copy(kv_ref.at[:, z], recv.at[:, z], own_sem)
    own.start()

    barrier = pltpu.get_barrier_semaphore()

    @pl.when(z > 0)
    def _():
        pl.semaphore_wait(barrier, 1)

    @pl.when(z < n - 1)
    def _():
        pl.semaphore_signal(barrier, inc=1, device_id={"seq": z + 1})

    def announce(s, carry):
        pl.semaphore_signal(ready.at[z], inc=1, device_id={"seq": s})
        return carry

    lax.fori_loop(0, z, announce, 0)

    def bulk(t, k, s=None):
        s = z if s is None else s
        return pltpu.make_async_remote_copy(
            src_ref=kv_ref.at[k, t],
            dst_ref=recv.at[k, s],
            send_sem=send_sem.at[k, t],
            recv_sem=recv_sem.at[k, s],
            device_id={"seq": t},
        )

    def send_part(t, carry):
        for k in range(kinds):
            bulk(t, k).start()
        return carry

    late = jnp.logical_and(z > half, z < n - 1)

    @pl.when(late)
    def _():
        send_part(0, 0)

    near = jnp.maximum(z - half + 1 - z % 2, 0)

    @pl.when(z < n - 1)
    def _():
        lax.fori_loop(near, z, send_part, 0)

    load.wait()

    def one_row(r, carry):
        k, u = r // users, r % users
        total = jnp.zeros((8, head_dim), jnp.float32)
        high = jnp.full((8, head_dim), -ceiling_value, jnp.float32)
        low = jnp.full((8, head_dim), ceiling_value, jnp.float32)
        count = blocks_ref[u]
        for b in range(per_dev):
            part = local[
                k,
                u * quarter + b // per_part,
                (b % per_part) * BLOCK : (b % per_part + 1) * BLOCK,
                :,
            ].astype(jnp.float32)
            part = part.reshape(BLOCK // 8, 8, head_dim)
            alive = z * per_dev + b < count
            total += jnp.where(alive, jnp.sum(part, axis=0), 0.0)
            high = jnp.maximum(high, jnp.where(alive, jnp.max(part, axis=0), -ceiling_value))
            low = jnp.minimum(low, jnp.where(alive, jnp.min(part, axis=0), ceiling_value))
        mine[0, pl.ds(r, 1), :] = jnp.sum(total, axis=0, keepdims=True)
        mine[1, pl.ds(r, 1), :] = jnp.max(high, axis=0, keepdims=True)
        mine[2, pl.ds(r, 1), :] = jnp.min(low, axis=0, keepdims=True)
        return carry

    lax.fori_loop(0, rows, one_row, 0)

    def prefix(s):
        return pltpu.make_async_remote_copy(
            src_ref=mine,
            dst_ref=gathered,
            send_sem=stat_send_sem,
            recv_sem=stat_recv_sem,
            device_id={"seq": s + 1},
        )

    @pl.when(z > 0)
    def _():
        prefix(z - 1).wait_recv()
        mine[0] = mine[0] + gathered[0]
        mine[1] = jnp.maximum(mine[1], gathered[1])
        mine[2] = jnp.minimum(mine[2], gathered[2])

    def final(t):
        return pltpu.make_async_remote_copy(
            src_ref=finals,
            dst_ref=finals,
            send_sem=final_send_sem.at[t],
            recv_sem=final_recv_sem,
            device_id={"seq": t},
        )

    @pl.when(z < n - 1)
    def _():
        pl.semaphore_wait(ready.at[z + 1], 1)
        prefix(z).start()

    @pl.when(z == n - 1)
    def _():
        row = lax.broadcasted_iota(jnp.int32, (rows, head_dim), 0)
        length = jnp.zeros((rows, head_dim), jnp.float32)
        for u in range(users):
            tokens = (blocks_ref[u] * BLOCK).astype(jnp.float32)
            length = jnp.where(row % users == u, tokens, length)
        center = mine[0] / length
        finals[0] = center
        finals[1] = jnp.maximum(mine[1] - center, center - mine[2]) + epsilon

        def send_final(t, carry):
            final(t).start()
            return carry

        lax.fori_loop(0, n - 1, send_final, 0)

    lax.fori_loop(jnp.where(late, 1, 0), near, send_part, 0)

    @pl.when(z == n - 1)
    def _():
        lax.fori_loop(near, z, send_part, 0)

    far = z + half + 1 - z % 2

    def send_upper(t, carry):
        @pl.when(t > z + 1)
        def _():
            pl.semaphore_wait(ready.at[t], 1)

        @pl.when(jnp.logical_or(z == 0, jnp.logical_or(z >= half, t < far)))
        def _():
            send_part(t, 0)

        return carry

    lax.fori_loop(z + 1, n, send_upper, 0)

    def in_turn():
        @pl.when(z > 0)
        def _():
            pl.semaphore_wait(token, 1)
            lax.fori_loop(far, n, send_part, 0)

        @pl.when(z < half - 1)
        def _():
            def drain_far(i, carry):
                bulk(i // kinds, i % kinds).wait_send()
                return carry

            lax.fori_loop(far * kinds, n * kinds - KEEP, drain_far, 0)
            pl.semaphore_signal(token, inc=1, device_id={"seq": z + 1})

    @pl.when(z < half // 2)
    def _():
        in_turn()

    @pl.when(z < n - 1)
    def _():
        final(z).wait_recv()

    my_count = blocks_ref[my_user]
    centers = [finals[0, pl.ds(k * users + my_user, 1), :] for k in range(kinds)]
    scales = [finals[1, pl.ds(k * users + my_user, 1), :] for k in range(kinds)]

    def normalise(s, carry):
        @pl.when(s == z)
        def _():
            own.wait()

        @pl.when(s != z)
        def _():
            for k in range(kinds):
                bulk(s, k, s).wait_recv()

        for k in range(kinds):
            for b in range(per_part):
                span = slice(b * BLOCK, (b + 1) * BLOCK)
                value = recv[k, s, span, :].astype(jnp.float32)
                scaled = (value - centers[k]) / scales[k]
                alive = s * per_dev + my_part * per_part + b < my_count
                done[k, s, span, :] = jnp.where(alive, scaled, 0.0).astype(done.dtype)
        pltpu.make_async_copy(done.at[:, s], out_ref.at[:, s], out_sem.at[s]).start()
        return carry

    lax.fori_loop(0, z + 1, normalise, 0)

    @pl.when(jnp.logical_and(z >= half // 2, early))
    def _():
        in_turn()

    for k in range(kinds):
        centers_ref[k] = finals[0, k * users : (k + 1) * users, :]
        scales_ref[k] = finals[1, k * users : (k + 1) * users, :]

    lax.fori_loop(z + 1, n, normalise, 0)

    @pl.when(z < n - 1)
    def _():
        prefix(z).wait_send()

    @pl.when(z == n - 1)
    def _():
        def drain_final(t, carry):
            final(t).wait_send()
            return carry

        lax.fori_loop(0, n - 1, drain_final, 0)

    def drain(t, carry):
        for k in range(kinds):
            waited = jnp.logical_and(
                jnp.logical_and(z < half - 1, t >= far), t * kinds + k < n * kinds - KEEP
            )

            @pl.when(jnp.logical_not(jnp.logical_or(waited, t == z)))
            def _(k=k):
                bulk(t, k).wait_send()

        pltpu.make_async_copy(done.at[:, t], out_ref.at[:, t], out_sem.at[t]).wait()
        return carry

    lax.fori_loop(0, n, drain, 0)


def on_device(kv_cache, valid_blocks):
    kinds, layer_dev, users, per_dev, heads_dev, head_dim = kv_cache.shape
    n = lax.axis_size("seq")
    part_len = per_dev // (n // users)
    kv = kv_cache.reshape(kinds, n, part_len, head_dim)
    whole = (kinds, n, part_len, head_dim)
    rows = kinds * users
    dma = pltpu.SemaphoreType.DMA
    out, centers, scales = pl.pallas_call(
        functools.partial(exchange_kernel, n),
        out_shape=(
            jax.ShapeDtypeStruct(whole, kv.dtype),
            jax.ShapeDtypeStruct((kinds, users, head_dim), jnp.float32),
            jax.ShapeDtypeStruct((kinds, users, head_dim), jnp.float32),
        ),
        in_specs=[
            pl.BlockSpec(memory_space=pl.ANY),
            pl.BlockSpec(memory_space=pltpu.SMEM),
        ],
        out_specs=(
            pl.BlockSpec(memory_space=pl.ANY),
            pl.BlockSpec(memory_space=pltpu.VMEM),
            pl.BlockSpec(memory_space=pltpu.VMEM),
        ),
        scratch_shapes=[
            pltpu.VMEM(whole, kv.dtype),
            pltpu.VMEM(whole, kv.dtype),
            pltpu.VMEM(whole, kv.dtype),
            pltpu.VMEM((3, rows, head_dim), jnp.float32),
            pltpu.VMEM((3, rows, head_dim), jnp.float32),
            pltpu.VMEM((2, rows, head_dim), jnp.float32),
            dma,
            dma,
            dma((n,)),
            dma((kinds, n)),
            dma((kinds, n)),
            dma,
            dma,
            dma((n,)),
            dma,
            pltpu.SemaphoreType.REGULAR((n,)),
            pltpu.SemaphoreType.REGULAR,
        ],
        compiler_params=pltpu.CompilerParams(collective_id=0, has_side_effects=True),
    )(kv, valid_blocks)
    arranged = out.reshape(kinds, layer_dev, 1, n * part_len, heads_dev, head_dim)
    small = (kinds, layer_dev, users, heads_dev, head_dim)
    return (arranged, centers.reshape(small), scales.reshape(small))


def solution(mesh):
    in_specs = (P(None, "layer", "groups", "seq", "head", None), P("groups"))
    out_specs = (
        P(None, "layer", ("groups", "seq"), None, "head", None),
        P(None, "layer", "groups", "head", None),
        P(None, "layer", "groups", "head", None),
    )
    return jax.shard_map(
        on_device, mesh=mesh, in_specs=in_specs, out_specs=out_specs, check_vma=False
    )
```

time: 135 us -> 122 us (0.904); the launches traced: 135 us -> 120 us
  Pallas kernels: 128 us -> 115 us
  other arithmetic: 3.17 us -> 0 us
  local copies, waits for them, and re-layouts: 2.54 us -> 4.24 us
    pallas_call x1, Pallas kernels: 128 us -> 115 us  [on_device(): pl.pallas_call(functools.partial(exchange_kernel, n), out_shape=(jax.Shap...]
    unnamed x2 -> x7, local copies, waits for them, and re-layouts: 0.01 us -> 4.24 us
    convert_element_type x1 -> x0, other arithmetic: 3.09 us -> none  [on_device(): normed.astype(kv_cache.dtype)]
where the time goes in v2:
time: 122 us; the launch traced here: 120 us
  Pallas kernels  115 us (94%)
  local copies, waits for them, and re-layouts  4.24 us (3%)
    pallas_call x1, Pallas kernels, on_device(): pl.pallas_call(functools.partial(exchange_kernel, n), out_shape=(jax.Shap...  115 us
    unnamed x7, local copies, waits for them, and re-layouts  4.24 us

profile of v2, /device:TPU:78, one launch (start us, length us, event | category | flops | bytes accessed | tf_op | source)
XLA Modules:
  0.0 120.0 jit_solution(16683008757705257942)
XLA Ops:
  0.6 115.1 %shard_map.49 = (bf16[2,16,256,128]{3,2,1,0:T(8,128)(2,1)}, f32[2,4,128]{2,1,0:T(4,128)}, f32[2,4,128]{2,1,0:T(4,128)}) custom-call(bf16[2,16,256,128]{3,2,1,0:T(8,128)(2,1)} %bitcast.10, s32[4]{0:T(128)} %blocks_ref.1), custom_call_target="tpu_custom_call" | custom-call | tf_op jit(solution)/shard_map/pallas_call | solution.py:291
  115.7 0.0 copy-start.1
  115.7 0.0 copy-start
  115.7 3.0 %copy.11 = bf16[2,1,1,4096,1,128]{5,3,4,2,1,0:T(8,128)(2,1)} copy(bf16[2,1,1,4096,1,128]{5,3,4,2,1,0:T(8,128)(2,1)} %bitcast.11) | data formatting | bytes 4194304
  118.8 0.0 copy-done.1
  118.8 0.6 copy.12
  119.4 0.0 copy-done
  119.4 0.6 copy.13
Async XLA Ops:
  115.7 3.1 %copy-start.1 = (f32[2,4,128]{2,1,0:T(4,128)S(1)}, f32[2,4,128]{2,1,0:T(4,128)}, u32[]{:S(2)}) copy-start(f32[2,4,128]{2,1,0:T(4,128)} %get-tuple-element.7) | copy-start | bytes 12292
  115.7 3.7 %copy-start = (f32[2,4,128]{2,1,0:T(4,128)S(1)}, f32[2,4,128]{2,1,0:T(4,128)}, u32[]{:S(2)}) copy-start(f32[2,4,128]{2,1,0:T(4,128)} %get-tuple-element.8) | copy-start | bytes 12292

commit v3 on v2

--- a/solution.py
+++ b/solution.py
@@ -11,7 +11,8 @@
 
 epsilon = 1e-06
 ceiling_value = 3e38
-KEEP = 2
+KEEP = (1, 2)
+VMEM_LIMIT = 51 * 1024 * 1024
 
 
 def exchange_kernel(
@@ -19,17 +20,14 @@
     kv_ref,
     blocks_ref,
     out_ref,
-    centers_ref,
-    scales_ref,
+    finals_ref,
     local,
     recv,
-    done,
     mine,
     gathered,
     finals,
     load_sem,
     own_sem,
-    out_sem,
     send_sem,
     recv_sem,
     stat_send_sem,
@@ -49,6 +47,7 @@
     z = lax.axis_index("seq")
     my_user, my_part = z // quarter, z % quarter
     early = z < half
+    keep = jnp.where(z == 0, KEEP[0], KEEP[1])
 
     load = pltpu.make_async_copy(kv_ref, local, load_sem)
     load.start()
@@ -86,7 +85,7 @@
             bulk(t, k).start()
         return carry
 
-    late = jnp.logical_and(z > half, z < n - 1)
+    late = jnp.logical_and(z >= half, z < n - 1)
 
     @pl.when(late)
     def _():
@@ -185,13 +184,14 @@
         def _():
             pl.semaphore_wait(ready.at[t], 1)
 
-        @pl.when(jnp.logical_or(z == 0, jnp.logical_or(z >= half, t < far)))
+        @pl.when(jnp.logical_and(early, jnp.logical_or(t <= half, jnp.logical_and(z == 0, t >= far))))
         def _():
             send_part(t, 0)
 
         return carry
 
     lax.fori_loop(z + 1, n, send_upper, 0)
+    lax.fori_loop(jnp.maximum(z, half) + 1, jnp.minimum(far, n), send_part, 0)
 
     def in_turn():
         @pl.when(z > 0)
@@ -205,7 +205,7 @@
                 bulk(i // kinds, i % kinds).wait_send()
                 return carry
 
-            lax.fori_loop(far * kinds, n * kinds - KEEP, drain_far, 0)
+            lax.fori_loop(far * kinds, n * kinds - keep, drain_far, 0)
             pl.semaphore_signal(token, inc=1, device_id={"seq": z + 1})
 
     @pl.when(z < half // 2)
@@ -236,8 +236,7 @@
                 value = recv[k, s, span, :].astype(jnp.float32)
                 scaled = (value - centers[k]) / scales[k]
                 alive = s * per_dev + my_part * per_part + b < my_count
-                done[k, s, span, :] = jnp.where(alive, scaled, 0.0).astype(done.dtype)
-        pltpu.make_async_copy(done.at[:, s], out_ref.at[:, s], out_sem.at[s]).start()
+                out_ref[k, s, span, :] = jnp.where(alive, scaled, 0.0).astype(out_ref.dtype)
         return carry
 
     lax.fori_loop(0, z + 1, normalise, 0)
@@ -246,9 +245,7 @@
     def _():
         in_turn()
 
-    for k in range(kinds):
-        centers_ref[k] = finals[0, k * users : (k + 1) * users, :]
-        scales_ref[k] = finals[1, k * users : (k + 1) * users, :]
+    finals_ref[...] = finals[...]
 
     lax.fori_loop(z + 1, n, normalise, 0)
 
@@ -267,14 +264,12 @@
     def drain(t, carry):
         for k in range(kinds):
             waited = jnp.logical_and(
-                jnp.logical_and(z < half - 1, t >= far), t * kinds + k < n * kinds - KEEP
+                jnp.logical_and(z < half - 1, t >= far), t * kinds + k < n * kinds - keep
             )
 
             @pl.when(jnp.logical_not(jnp.logical_or(waited, t == z)))
             def _(k=k):
                 bulk(t, k).wait_send()
-
-        pltpu.make_async_copy(done.at[:, t], out_ref.at[:, t], out_sem.at[t]).wait()
         return carry
 
     lax.fori_loop(0, n, drain, 0)
@@ -288,32 +283,28 @@
     whole = (kinds, n, part_len, head_dim)
     rows = kinds * users
     dma = pltpu.SemaphoreType.DMA
-    out, centers, scales = pl.pallas_call(
+    out, finals = pl.pallas_call(
         functools.partial(exchange_kernel, n),
         out_shape=(
             jax.ShapeDtypeStruct(whole, kv.dtype),
-            jax.ShapeDtypeStruct((kinds, users, head_dim), jnp.float32),
-            jax.ShapeDtypeStruct((kinds, users, head_dim), jnp.float32),
+            jax.ShapeDtypeStruct((2, rows, head_dim), jnp.float32),
         ),
         in_specs=[
             pl.BlockSpec(memory_space=pl.ANY),
             pl.BlockSpec(memory_space=pltpu.SMEM),
         ],
         out_specs=(
-            pl.BlockSpec(memory_space=pl.ANY),
             pl.BlockSpec(memory_space=pltpu.VMEM),
             pl.BlockSpec(memory_space=pltpu.VMEM),
         ),
         scratch_shapes=[
             pltpu.VMEM(whole, kv.dtype),
             pltpu.VMEM(whole, kv.dtype),
-            pltpu.VMEM(whole, kv.dtype),
             pltpu.VMEM((3, rows, head_dim), jnp.float32),
             pltpu.VMEM((3, rows, head_dim), jnp.float32),
             pltpu.VMEM((2, rows, head_dim), jnp.float32),
             dma,
             dma,
-            dma((n,)),
             dma((kinds, n)),
             dma((kinds, n)),
             dma,
@@ -323,11 +314,11 @@
             pltpu.SemaphoreType.REGULAR((n,)),
             pltpu.SemaphoreType.REGULAR,
         ],
-        compiler_params=pltpu.CompilerParams(collective_id=0, has_side_effects=True),
+        compiler_params=pltpu.CompilerParams(collective_id=0, has_side_effects=True, vmem_limit_bytes=VMEM_LIMIT),
     )(kv, valid_blocks)
     arranged = out.reshape(kinds, layer_dev, 1, n * part_len, heads_dev, head_dim)
     small = (kinds, layer_dev, users, heads_dev, head_dim)
-    return (arranged, centers.reshape(small), scales.reshape(small))
+    return (arranged, finals[0].reshape(small), finals[1].reshape(small))
 
 
 def solution(mesh):

time: 122 us -> 120 us (0.984)
  the two profiles are of different devices: /device:TPU:78 before, /device:TPU:1344 now
where the time goes in v3:
time: 120 us
  Pallas kernels  116 us (97%)
  local copies, waits for them, and re-layouts  2.57 us (2%)
    pallas_call x1, Pallas kernels, on_device(): pl.pallas_call(functools.partial(exchange_kernel, n), out_shape=(jax.Shap...  116 us

profile of v3, /device:TPU:1344, one launch (start us, length us, event | category | flops | bytes accessed | tf_op | source)
XLA Modules:
  0.0 119.7 jit_solution(8545436090161247364)
XLA Ops:
  0.6 0.0 copy-start
  0.6 0.6 copy-done
  1.3 116.5 %shard_map.49 = (bf16[2,16,256,128]{3,2,1,0:T(8,128)(2,1)S(1)}, f32[2,8,128]{2,1,0:T(8,128)S(1)}) custom-call(bf16[2,16,256,128]{3,2,1,0:T(8,128)(2,1)} %bitcast.11, s32[4]{0:T(128)S(1)} %copy-done), custom_call_target="tpu_custom_call" | custom-call | tf_op jit(solution)/shard_map/pallas_call | solution.py:286
  117.7 0.6 fusion
  118.3 1.3 %copy.9 = bf16[2,1,1,4096,1,128]{5,3,4,2,1,0:T(8,128)(2,1)} copy(bf16[2,1,1,4096,1,128]{5,3,4,2,1,0:T(8,128)(2,1)S(1)} %bitcast.10) | data formatting | bytes 4194304
Async XLA Ops:
  0.6 0.7 copy-start

commit v4 on v3

--- a/solution.py
+++ b/solution.py
@@ -188,10 +188,16 @@
         def _():
             send_part(t, 0)
 
+        release = n - quarter
+        begin = jnp.where(t > release, t, jnp.maximum(z, half) + 1)
+
+        @pl.when(t >= release)
+        def _():
+            lax.fori_loop(begin, jnp.minimum(far, t + 1), send_part, 0)
+
         return carry
 
     lax.fori_loop(z + 1, n, send_upper, 0)
-    lax.fori_loop(jnp.maximum(z, half) + 1, jnp.minimum(far, n), send_part, 0)
 
     def in_turn():
         @pl.when(z > 0)

time: 120 us -> 120 us (level)
  no operation moved by 1% of the time
where the time goes in v4:
time: 120 us
  Pallas kernels  116 us (97%)
  local copies, waits for them, and re-layouts  2.57 us (2%)
    pallas_call x1, Pallas kernels, on_device(): pl.pallas_call(functools.partial(exchange_kernel, n), out_shape=(jax.Shap...  116 us

profile of v4, /device:TPU:1344, one launch (start us, length us, event | category | flops | bytes accessed | tf_op | source)
XLA Modules:
  0.0 119.6 jit_solution(9228946827332678055)
XLA Ops:
  0.6 0.0 copy-start
  0.6 0.6 copy-done
  1.3 116.3 %shard_map.49 = (bf16[2,16,256,128]{3,2,1,0:T(8,128)(2,1)S(1)}, f32[2,8,128]{2,1,0:T(8,128)S(1)}) custom-call(bf16[2,16,256,128]{3,2,1,0:T(8,128)(2,1)} %bitcast.11, s32[4]{0:T(128)S(1)} %copy-done), custom_call_target="tpu_custom_call" | custom-call | tf_op jit(solution)/shard_map/pallas_call | solution.py:292
  117.6 0.6 fusion
  118.2 1.3 %copy.9 = bf16[2,1,1,4096,1,128]{5,3,4,2,1,0:T(8,128)(2,1)} copy(bf16[2,1,1,4096,1,128]{5,3,4,2,1,0:T(8,128)(2,1)S(1)} %bitcast.10) | data formatting | bytes 4194304
Async XLA Ops:
  0.6 0.7 copy-start
